TPU v7x, 32 devices: a whole 2x2x4 slice. The times are simulated.
32 devices in a mesh: subj: 4 (over y, x), cortex: 8 (over z, core).
Axes of the slice: x: 2, y: 2, z: 4, core: 2. Of those that a mesh axis runs over, the one named last changes fastest.
Arguments:
- series: bfloat16 [8, 1024, 2048], P('subj', None, 'cortex'), may hold values from -6 to 6
- template: bfloat16 [1024, 2048], P(None, 'cortex'), may hold values from -6 to 6
- sl_blocks: int32 [16, 3], P('cortex'), may hold values from 0 to 15, as said below
Outputs:
- template_new: float32 [1024, 2048], P(None, 'cortex')
Inputs may be any that keep to these rules, and one draw needn't show every extreme that they name: sl_blocks[g, 0] = g; the other two entries of row g are distinct, differ from g, and lie between (g // 2 - 1) * 2 and (g // 2 + 2) * 2 - 1.
All inputs are finite; a program needn't handle non-finite values.
Results may differ from a plain program's by a relative error of at most 0.0024.
Values may be sent and summed in bfloat16 or wider, within the bound.
No kernel may reach another device: no remote copies, remote signals or barrier semaphores. Data moves between devices by JAX's collectives and lax.ppermute only.
A program may use at most 64 MiB of HBM per device.

v0:
```python
import jax
import jax.numpy as jnp
from jax import lax
from jax.sharding import PartitionSpec as P

BLOCK = 128
NS_STEPS = 8
BLK_DEV = 2
RIDGE_SHIFT = 0.1
NORM_EPSILON = 1e-06


def with_halo(cells, sides, width):
    for axis, dim in sides:
        count = lax.axis_size(axis)
        ends = count - 1
        head = lax.slice_in_dim(cells, 0, width, axis=dim)
        tail = lax.slice_in_dim(cells, cells.shape[dim] - width, cells.shape[dim], axis=dim)
        cells = jnp.concatenate(
            [
                lax.ppermute(tail, axis, [(i, (i + 1) % count) for i in range(ends)]),
                cells,
                lax.ppermute(head, axis, [((i + 1) % count, i) for i in range(ends)]),
            ],
            axis=dim,
        )
    return cells


def from_behind(block, axis, distance):
    devices = range(lax.axis_size(axis))
    route = [(i - distance, i) for i in devices if i - distance in devices]
    return lax.ppermute(block, axis, route)


def body(series, template, sl_blocks):
    subj_count = series.shape[0]
    frame_count = series.shape[1]
    width_dev = series.shape[2]
    halo_data = with_halo(series, (("cortex", 2),), width_dev)
    halo_tmpl = with_halo(template, (("cortex", 1),), width_dev)
    all_lists = lax.all_gather(sl_blocks, "cortex", axis=0, tiled=True)
    position = lax.axis_index("cortex")
    window_blocks = 3 * BLK_DEV
    window_ids = (sl_blocks - (position - 1) * BLK_DEV).reshape(-1)
    data_blocks = halo_data.reshape(subj_count, frame_count, window_blocks, BLOCK)
    tmpl_blocks = halo_tmpl.reshape(frame_count, window_blocks, BLOCK)
    subj_tiles = jnp.take(data_blocks, window_ids, axis=2).reshape(
        subj_count, frame_count, BLK_DEV, 3 * BLOCK
    )
    tmpl_tiles = jnp.take(tmpl_blocks, window_ids, axis=1).reshape(frame_count, BLK_DEV, 3 * BLOCK)
    identity = jnp.eye(3 * BLOCK, dtype=jnp.float32)
    cross_prod = jnp.einsum(
        "sfka,fkb->skab", subj_tiles, tmpl_tiles, preferred_element_type=jnp.float32
    )
    cross_prod = cross_prod / frame_count + RIDGE_SHIFT * identity
    squares = jnp.sum(cross_prod * cross_prod, axis=(2, 3), keepdims=True)
    polar_map = (cross_prod / jnp.sqrt(squares + NORM_EPSILON)).astype(jnp.bfloat16)
    for iteration in range(NS_STEPS):
        gram_mat = jnp.einsum(
            "skab,skac->skbc", polar_map, polar_map, preferred_element_type=jnp.float32
        ).astype(jnp.bfloat16)
        product = jnp.einsum(
            "skab,skbc->skac", polar_map, gram_mat, preferred_element_type=jnp.float32
        )
        polar_map = (1.5 * polar_map.astype(jnp.float32) - 0.5 * product).astype(jnp.bfloat16)
    mapped = jnp.einsum(
        "sfka,skab->sfkb", subj_tiles, polar_map, preferred_element_type=jnp.float32
    )
    tiles = mapped.reshape(subj_count, frame_count, BLK_DEV * 3, BLOCK)
    one_hot = (window_ids[:, None] == jnp.arange(window_blocks, dtype=jnp.int32)[None, :]).astype(
        jnp.float32
    )
    window_sum = jnp.einsum("sfjc,jw->sfwc", tiles, one_hot, precision=lax.Precision.HIGHEST)
    window_sum = window_sum.reshape(subj_count, frame_count, 3, width_dev)
    mine = position * BLK_DEV + jnp.arange(BLK_DEV, dtype=jnp.int32)
    block_ids = all_lists.reshape(-1)
    coverage = jnp.sum((block_ids[:, None] == mine[None, :]).astype(jnp.float32), axis=0)
    per_vertex = jnp.repeat(coverage, BLOCK)
    subject_sum = jnp.sum(window_sum, axis=0)
    from_lower = from_behind(subject_sum[:, 2].astype(jnp.bfloat16), "cortex", 1).astype(
        jnp.float32
    )
    from_upper = from_behind(subject_sum[:, 0].astype(jnp.bfloat16), "cortex", -1).astype(
        jnp.float32
    )
    own_sum = subject_sum[:, 1] + from_lower + from_upper
    averaged = own_sum / per_vertex[None, :]
    combined = lax.psum(averaged, "subj")
    return combined / (subj_count * lax.axis_size("subj"))


def solution(mesh):
    in_specs = (P("subj", None, "cortex"), P(None, "cortex"), P("cortex", None))
    out_specs = P(None, "cortex")
    return jax.shard_map(body, mesh=mesh, in_specs=in_specs, out_specs=out_specs, check_vma=False)
```

profile of v0, /device:TPU:0, one launch (start us, length us, event | category | flops | bytes accessed | tf_op | source)
XLA Modules:
  0.0 178.3 jit_solution(3251400548601477879)
XLA Ops:
  6.5 1.3 copy.147
  7.9 1.3 collective-permute-start.1
  9.2 3.8 %collective-permute-start = (bf16[1024,256]{0,1:T(8,128)(2,1)S(1)}, bf16[1024,256]{0,1:T(8,128)(2,1)}, u32[]{:S(2)}, u32[]{:S(2)}) collective-permute-start(bf16[1024,256]{0,1:T(8,128)(2,1)S(1)} %copy.147), channel_id=1, source_target_pairs={{0,1},{1,2},{2,3},{3,4},{4,5},{5,6},{6,7},{8,9},{9,10},{10,11},{11... | collective-permute-start | bytes 1572872 | tf_op jit(solution)/shard_map/ppermute | solution.py:21
  13.0 1.3 copy.152
  14.3 1.3 collective-permute-start.3
  15.6 5.4 %collective-permute-start.2 = (bf16[2,1024,256]{1,2,0:T(8,128)(2,1)}, bf16[2,1024,256]{1,2,0:T(8,128)(2,1)}, u32[]{:S(2)}, u32[]{:S(2)}) collective-permute-start(bf16[2,1024,256]{1,2,0:T(8,128)(2,1)} %copy.152), channel_id=1, source_target_pairs={{0,1},{1,2},{2,3},{3,4},{4,5},{5,6},{6,7},{8,9},{9,10},{10,11},{11... | collective-permute-start | bytes 3145736 | tf_op jit(solution)/shard_map/ppermute | solution.py:21
  21.1 0.1 broadcast_bitcast_fusion
  21.1 0.1 reshape.82
  21.2 0.1 eq.37
  21.3 0.9 fusion.24
  22.2 0.0 collective-permute-done.1
  22.2 0.8 copy-done.3
  23.0 0.0 collective-permute-done
  23.0 1.3 pad_maximum_fusion.1
  24.3 0.9 copy.150
  25.2 0.8 gather_fusion
  26.1 0.7 copy.151
  26.8 1.4 bitcast_select_fusion.1
  28.2 0.0 collective-permute-done.3
  28.2 0.0 collective-permute-done.2
  28.2 3.1 %pad_maximum_fusion = bf16[2,1024,768]{1,2,0:T(8,128)(2,1)} fusion(bf16[2,1024,256]{1,2,0:T(8,128)(2,1)} %collective-permute-done.3, bf16[2,1024,256]{1,2,0:T(8,128)(2,1)} %copy.152, bf16[2,1024,256]{1,2,0:T(8,128)(2,1)} %collective-permute-done.2), kind=kLoop, calls=%fused_computation.2 | loop fusion | flops 9437184 | bytes 6291456 | tf_op jit(solution)/shard_map/concatenate | solution.py:19
  31.3 3.5 %copy.155 = bf16[2,1024,6,128]{3,1,2,0:T(8,128)(2,1)S(1)} copy(bf16[2,1024,6,128]{1,3,2,0:T(8,128)(2,1)} %bitcast.72) | data formatting | bytes 6291456 | tf_op jit(solution)/shard_map/reshape | solution.py:46
  34.8 2.7 %gather_fusion.1 = bf16[6,2,1024,128]{3,2,1,0:T(8,128)(2,1)} fusion(bf16[2,1024,6,128]{3,1,2,0:T(8,128)(2,1)S(1)} %copy.155, s32[1024]{0:T(1024)S(1)} %pad_clamp_fusion), kind=kCustom, calls=%fused_computation.1 | custom fusion | bytes 6291480 | tf_op jit(solution)/shard_map/jit(_take)/gather | solution.py:48
  37.5 3.4 %copy.156 = bf16[2,1024,6,128]{1,3,2,0:T(8,128)(2,1)S(1)} copy(bf16[2,1024,6,128]{3,1,0,2:T(8,128)(2,1)} %bitcast.70) | data formatting | bytes 6291456 | tf_op jit(solution)/shard_map/jit(_take)/gather | solution.py:48
  40.9 0.3 bitcast_select_fusion
  41.3 0.7 copy-done
  42.0 0.5 copy-done.1
  42.5 1.7 multiply_reduce_fusion
  44.1 0.5 divide_convert_fusion
  44.7 0.9 convolution_convert_fusion.7
  45.6 1.0 subtract_convert_fusion.7
  46.6 0.9 convolution_convert_fusion.6
  47.5 1.0 subtract_convert_fusion.6
  48.5 0.9 convolution_convert_fusion.5
  49.5 1.0 subtract_convert_fusion.5
  50.4 0.9 convolution_convert_fusion.4
  51.4 1.0 subtract_convert_fusion.4
  52.4 0.9 convolution_convert_fusion.3
  53.3 1.0 subtract_convert_fusion.3
  54.3 0.9 convolution_convert_fusion.2
  55.2 1.2 subtract_convert_fusion.2
  56.4 0.9 convolution_convert_fusion.1
  57.4 1.0 subtract_convert_fusion.1
  58.4 0.9 convolution_convert_fusion
  59.3 1.0 subtract_convert_fusion
  60.3 4.5 %fusion.10 = f32[2,2,384,1024]{3,2,1,0:T(8,128)} fusion(bf16[2,1024,2,384]{1,3,2,0:T(8,128)(2,1)S(1)} %bitcast_select_fusion, bf16[2,2,384,384]{2,3,0,1:T(8,128)(2,1)S(1)} %subtract_convert_fusion), kind=kOutput, calls=%fused_computation.36 | convolution fusion | flops 1207959552 | bytes 10616832 | tf_op jit(solution)/shard_map/sfka,skab->sfkb/dot_general | solution.py:67
  64.8 8.2 %copy.193 = f32[2,1024,6,128]{3,2,1,0:T(8,128)} copy(f32[2,1024,6,128]{1,3,2,0:T(8,128)} %bitcast.67) | data formatting | bytes 12582912 | tf_op jit(solution)/shard_map/reshape | solution.py:70
  73.0 10.4 %convolution_reduce_fusion = f32[6,1024,128]{2,0,1:T(8,128)} fusion(f32[2,1024,6,128]{3,2,1,0:T(8,128)} %copy.193, s32[6]{0:T(128)S(1)} %eq.37), kind=kOutput, calls=%fused_computation.6 | convolution fusion | flops 114032672 | bytes 9437208 | tf_op jit(solution)/shard_map/sfjc,jw->sfwc/dot_general | solution.py:74
  83.5 3.7 %copy.194 = f32[1024,6,128]{0,2,1:T(8,128)S(1)} copy(f32[1024,6,128]{2,1,0:T(8,128)} %bitcast.71) | data formatting | bytes 6291456 | tf_op jit(solution)/shard_map/reduce_sum | solution.py:80
  87.2 0.2 bitcast_convert_fusion
  87.4 1.0 slice_bitcast_fusion.2
  88.4 8.4 %collective-permute-start.4 = (bf16[1024,256]{0,1:T(8,128)(2,1)}, bf16[1024,256]{0,1:T(8,128)(2,1)}, u32[]{:S(2)}, u32[]{:S(2)}) collective-permute-start(bf16[1024,256]{0,1:T(8,128)(2,1)} %get-tuple-element.7), channel_id=1, source_target_pairs={{0,1},{1,2},{2,3},{3,4},{4,5},{5,6},{6,7},{8,9},{9,10},{10,11},{11... | collective-permute-start | bytes 1572872 | tf_op jit(solution)/shard_map/ppermute | solution.py:33
  96.8 1.3 collective-permute-start.5
  98.1 15.2 %all-gather = s32[8,2,3]{2,1,0:T(2,128)S(1)} all-gather(s32[1,2,3]{2,1,0:T(2,128)S(1)} %bitcast.79), channel_id=1, replica_groups=mesh['subj'=4,'cortex'=8] {'cortex'}, dimensions={0}, use_global_device_ids=true | all-gather | bytes 216 | tf_op jit(solution)/shard_map/all_gather | solution.py:42
  113.3 0.1 eq.42
  113.4 0.2 fusion.28
  113.5 0.1 broadcast_bitcast_fusion.1
  113.6 0.0 collective-permute-done.4
  113.6 0.0 collective-permute-done.5
  113.6 2.4 %fusion.23 = f32[1024,256]{0,1:T(8,128)} fusion(f32[1024,3,256]{0,2,1:T(8,128)S(1)} %bitcast.69, bf16[1024,256]{0,1:T(8,128)(2,1)} %collective-permute-done.5, bf16[1024,256]{0,1:T(8,128)(2,1)} %collective-permute-done.4, f32[256]{0:T(256)S(1)} %broadcast_bitcast_fusion.1), kind=kLoop, calls=%fused_computation.50 | loop fusion | flops 1310720 | bytes 3146752 | tf_op jit(solution)/shard_map/div | solution.py:88
  116.0 0.0 all-reduce.2.cloned.1.call-update
  116.0 52.8 %all-reduce.2.cloned.1.call-done = f32[1024,256]{0,1:T(8,128)} async-done(((f32[1024,256]{0,1:T(8,128)}), f32[1024,256]{0,1:T(8,128)}) %all-reduce.2.cloned.1.call-update) | async-done | bytes 1048592 | tf_op jit(solution)/shard_map/psum | solution.py:89
  168.9 1.3 broadcast_multiply_fusion
  170.2 1.3 copy.195
  (14 shorter events, 0.1 us)
Async XLA Ops:
  6.5 6.5 %copy-start.2 = (bf16[2,1024,256]{2,1,0:T(8,128)(2,1)S(1)}, bf16[2,1024,256]{2,1,0:T(8,128)(2,1)}, u32[]{:S(2)}) copy-start(bf16[2,1024,256]{2,1,0:T(8,128)(2,1)} %param.3) | copy-start | bytes 3145732
  6.5 14.5 %copy-start.4 = (s32[2,3]{1,0:T(2,128)S(1)}, s32[2,3]{1,0:T(2,128)}, u32[]{:S(2)}) copy-start(s32[2,3]{1,0:T(2,128)} %param.5) | copy-start | bytes 76
  6.5 162.3 %all-reduce.2.cloned.1.call-start = ((), (), s32[]{:S(2)}) async-start(), calls=%async_computation | async-start | bytes 2097152 | tf_op jit(solution)/shard_map/psum | solution.py:89
  7.9 14.3 %collective-permute-start.1 = (bf16[1024,256]{0,1:T(8,128)(2,1)S(1)}, bf16[1024,256]{0,1:T(8,128)(2,1)S(1)}, u32[]{:S(2)}, u32[]{:S(2)}) collective-permute-start(bf16[1024,256]{0,1:T(8,128)(2,1)S(1)} %copy.147), channel_id=1, source_target_pairs={{1,0},{2,1},{3,2},{4,3},{5,4},{6,5},{7,6},{9,8},{10,9},{11,10},{12... | collective-permute-start | bytes 1572872 | tf_op jit(solution)/shard_map/ppermute | solution.py:23
  9.2 13.8 %collective-permute-start = (bf16[1024,256]{0,1:T(8,128)(2,1)S(1)}, bf16[1024,256]{0,1:T(8,128)(2,1)}, u32[]{:S(2)}, u32[]{:S(2)}) collective-permute-start(bf16[1024,256]{0,1:T(8,128)(2,1)S(1)} %copy.147), channel_id=1, source_target_pairs={{0,1},{1,2},{2,3},{3,4},{4,5},{5,6},{6,7},{8,9},{9,10},{10,11},{11... | collective-permute-start | bytes 1572872 | tf_op jit(solution)/shard_map/ppermute | solution.py:21
  14.3 13.8 %collective-permute-start.3 = (bf16[2,1024,256]{1,2,0:T(8,128)(2,1)}, bf16[2,1024,256]{1,2,0:T(8,128)(2,1)}, u32[]{:S(2)}, u32[]{:S(2)}) collective-permute-start(bf16[2,1024,256]{1,2,0:T(8,128)(2,1)} %copy.152), channel_id=1, source_target_pairs={{1,0},{2,1},{3,2},{4,3},{5,4},{6,5},{7,6},{9,8},{10,9},{11,10},{12... | collective-permute-start | bytes 3145736 | tf_op jit(solution)/shard_map/ppermute | solution.py:23
  15.6 12.6 %collective-permute-start.2 = (bf16[2,1024,256]{1,2,0:T(8,128)(2,1)}, bf16[2,1024,256]{1,2,0:T(8,128)(2,1)}, u32[]{:S(2)}, u32[]{:S(2)}) collective-permute-start(bf16[2,1024,256]{1,2,0:T(8,128)(2,1)} %copy.152), channel_id=1, source_target_pairs={{0,1},{1,2},{2,3},{3,4},{4,5},{5,6},{6,7},{8,9},{9,10},{10,11},{11... | collective-permute-start | bytes 3145736 | tf_op jit(solution)/shard_map/ppermute | solution.py:21
  22.2 0.8 copy-start.3
  40.9 1.1 copy-start
  40.9 1.6 copy-start.1
  88.4 25.2 %collective-permute-start.4 = (bf16[1024,256]{0,1:T(8,128)(2,1)}, bf16[1024,256]{0,1:T(8,128)(2,1)}, u32[]{:S(2)}, u32[]{:S(2)}) collective-permute-start(bf16[1024,256]{0,1:T(8,128)(2,1)} %get-tuple-element.7), channel_id=1, source_target_pairs={{0,1},{1,2},{2,3},{3,4},{4,5},{5,6},{6,7},{8,9},{9,10},{10,11},{11... | collective-permute-start | bytes 1572872 | tf_op jit(solution)/shard_map/ppermute | solution.py:33
  96.8 16.8 %collective-permute-start.5 = (bf16[1024,256]{0,1:T(8,128)(2,1)}, bf16[1024,256]{0,1:T(8,128)(2,1)}, u32[]{:S(2)}, u32[]{:S(2)}) collective-permute-start(bf16[1024,256]{0,1:T(8,128)(2,1)} %get-tuple-element.8), channel_id=1, source_target_pairs={{1,0},{2,1},{3,2},{4,3},{5,4},{6,5},{7,6},{9,8},{10,9},{11,10},{12... | collective-permute-start | bytes 1572872 | tf_op jit(solution)/shard_map/ppermute | solution.py:33
Sparse Core Ops, SparseCore 0:
  116.2 52.6 all-reduce.1
where the time goes:
time: 179 us; the launch traced here: 178 us
  waiting for transfers between devices  52.9 us (30%)
  matrix products  32.1 us (18%)
  local copies, waits for them, and re-layouts  31.3 us (17%)
  starting transfers between devices  21.5 us (12%)
  blocking collectives  15.2 us (8%)
  between operations  13.7 us (8%)
  other arithmetic  11.7 us (7%)
    psum x1, waiting for transfers between devices, body(): combined = lax.psum(averaged, 'subj')  52.8 us
    all_gather x1, blocking collectives, body(): all_lists = lax.all_gather(sl_blocks, 'cortex', axis=0, tiled=True)  15.2 us
    dot_general x1, matrix products, body(): jnp.einsum('sfjc,jw->sfwc', tiles, one_hot, precision=lax.Precision.HIGHEST)  10.4 us
    ppermute x2, starting transfers between devices, from_behind(): return lax.ppermute(block, axis, route)  9.64 us
    ppermute x2, starting transfers between devices, with_halo(): lax.ppermute(tail, axis, [(i, (i + 1) % count) for i in range(ends)])  9.27 us
    reshape x1, local copies, waits for them, and re-layouts, body(): tiles = mapped.reshape(subj_count, frame_count, BLK_DEV * 3, BLOCK)  8.21 us
    dot_general x8, matrix products, body(): jnp.einsum('skab,skbc->skac', polar_map, gram_mat, preferred_element_type...  8.04 us
    dot_general x8, matrix products, body(): jnp.einsum('skab,skac->skbc', polar_map, polar_map, preferred_element_typ...  7.46 us
  transfers between devices with their start and end apart: 7, of which 1 were waited for; matrix products, arithmetic and copies ran while one was open for 4% of the time, Pallas kernels for 0%

commit v1 on v0

--- a/solution.py
+++ b/solution.py
@@ -39,7 +39,14 @@
     width_dev = series.shape[2]
     halo_data = with_halo(series, (("cortex", 2),), width_dev)
     halo_tmpl = with_halo(template, (("cortex", 1),), width_dev)
-    all_lists = lax.all_gather(sl_blocks, "cortex", axis=0, tiled=True)
+    ring = [sl_blocks]
+    for hop in range(7):
+        ring.append(lax.ppermute(ring[-1], "cortex", [(dev, (dev + 1) % 8) for dev in range(8)]))
+    all_lists = jnp.roll(
+        jnp.concatenate(ring[::-1], axis=0),
+        (lax.axis_index("cortex") + 1) * ring[0].shape[0],
+        axis=0,
+    )
     position = lax.axis_index("cortex")
     window_blocks = 3 * BLK_DEV
     window_ids = (sl_blocks - (position - 1) * BLK_DEV).reshape(-1)

time: 179 us -> 193 us (1.078)
  waiting for transfers between devices: 52.9 us -> 78.8 us
  blocking collectives: 15.2 us -> 0 us
  starting transfers between devices: 21.5 us -> 24.1 us
    ppermute x0 -> x7, waiting for transfers between devices: none -> 27.9 us  [body(): lax.ppermute(ring[-1], 'cortex', [(dev, (dev + 1) % 8) for dev in range(8)])]
    all_gather x1 -> x0, blocking collectives: 15.2 us -> none  [body(): all_lists = lax.all_gather(sl_blocks, 'cortex', axis=0, tiled=True)]
    ppermute x0 -> x7, starting transfers between devices: none -> 3.41 us  [body(): lax.ppermute(ring[-1], 'cortex', [(dev, (dev + 1) % 8) for dev in range(8)])]
    psum x1, waiting for transfers between devices: 52.8 us -> 50.8 us  [body(): combined = lax.psum(averaged, 'subj')]
    unnamed x14 -> x15, local copies, waits for them, and re-layouts: 4.75 us -> 4.85 us
  transfers between devices with their start and end apart: 7 -> 14, of which waited for: 1 -> 7; matrix products, arithmetic and copies ran while one was open for 4% -> 35% of each run, Pallas kernels for 0% -> 0%
where the time goes in v1:
time: 193 us; the launch traced here: 192 us
  waiting for transfers between devices  78.8 us (41%)
  matrix products  32.1 us (17%)
  local copies, waits for them, and re-layouts  31.7 us (16%)
  starting transfers between devices  24.1 us (12%)
  between operations  13.7 us (7%)
  other arithmetic  11.7 us (6%)
    psum x1, waiting for transfers between devices, body(): combined = lax.psum(averaged, 'subj')  50.8 us
    ppermute x7, waiting for transfers between devices, body(): lax.ppermute(ring[-1], 'cortex', [(dev, (dev + 1) % 8) for dev in range(8)])  27.9 us
    dot_general x1, matrix products, body(): jnp.einsum('sfjc,jw->sfwc', tiles, one_hot, precision=lax.Precision.HIGHEST)  10.4 us
    ppermute x2, starting transfers between devices, with_halo(): lax.ppermute(tail, axis, [(i, (i + 1) % count) for i in range(ends)])  9.27 us
    ppermute x2, starting transfers between devices, from_behind(): return lax.ppermute(block, axis, route)  8.81 us
    reshape x1, local copies, waits for them, and re-layouts, body(): tiles = mapped.reshape(subj_count, frame_count, BLK_DEV * 3, BLOCK)  8.21 us
    dot_general x8, matrix products, body(): jnp.einsum('skab,skbc->skac', polar_map, gram_mat, preferred_element_type...  8.04 us
    dot_general x8, matrix products, body(): jnp.einsum('skab,skac->skbc', polar_map, polar_map, preferred_element_typ...  7.46 us
  transfers between devices with their start and end apart: 14, of which 7 were waited for; matrix products, arithmetic and copies ran while one was open for 35% of the time, Pallas kernels for 0%

profile of v1, /device:TPU:0, one launch (start us, length us, event | category | flops | bytes accessed | tf_op | source)
XLA Modules:
  0.0 192.0 jit_solution(4701261328644621650)
XLA Ops:
  6.5 1.3 copy.151
  7.9 1.3 collective-permute-start.1
  9.2 3.8 %collective-permute-start = (bf16[1024,256]{0,1:T(8,128)(2,1)S(1)}, bf16[1024,256]{0,1:T(8,128)(2,1)}, u32[]{:S(2)}, u32[]{:S(2)}) collective-permute-start(bf16[1024,256]{0,1:T(8,128)(2,1)S(1)} %copy.151), channel_id=1, source_target_pairs={{0,1},{1,2},{2,3},{3,4},{4,5},{5,6},{6,7},{8,9},{9,10},{10,11},{11... | collective-permute-start | bytes 1572872 | tf_op jit(solution)/shard_map/ppermute | solution.py:21
  13.0 1.3 copy.156
  14.3 1.3 collective-permute-start.3
  15.6 5.4 %collective-permute-start.2 = (bf16[2,1024,256]{1,2,0:T(8,128)(2,1)}, bf16[2,1024,256]{1,2,0:T(8,128)(2,1)}, u32[]{:S(2)}, u32[]{:S(2)}) collective-permute-start(bf16[2,1024,256]{1,2,0:T(8,128)(2,1)} %copy.156), channel_id=1, source_target_pairs={{0,1},{1,2},{2,3},{3,4},{4,5},{5,6},{6,7},{8,9},{9,10},{10,11},{11... | collective-permute-start | bytes 3145736 | tf_op jit(solution)/shard_map/ppermute | solution.py:21
  21.1 0.1 copy.199
  21.1 0.7 collective-permute-start.6
  22.2 0.8 fusion.24
  23.0 0.8 copy-done.3
  23.8 1.3 pad_maximum_fusion.1
  25.1 0.9 copy.154
  26.0 0.8 gather_fusion
  26.9 0.7 copy.155
  27.6 1.4 bitcast_select_fusion.1
  29.0 3.1 %pad_maximum_fusion = bf16[2,1024,768]{1,2,0:T(8,128)(2,1)} fusion(bf16[2,1024,256]{1,2,0:T(8,128)(2,1)} %collective-permute-done.3, bf16[2,1024,256]{1,2,0:T(8,128)(2,1)} %copy.156, bf16[2,1024,256]{1,2,0:T(8,128)(2,1)} %collective-permute-done.2), kind=kLoop, calls=%fused_computation.2 | loop fusion | flops 9437184 | bytes 6291456 | tf_op jit(solution)/shard_map/concatenate | solution.py:19
  32.1 3.5 %copy.159 = bf16[2,1024,6,128]{3,1,2,0:T(8,128)(2,1)S(1)} copy(bf16[2,1024,6,128]{1,3,2,0:T(8,128)(2,1)} %bitcast.71) | data formatting | bytes 6291456 | tf_op jit(solution)/shard_map/reshape | solution.py:53
  35.6 2.7 %gather_fusion.1 = bf16[6,2,1024,128]{3,2,1,0:T(8,128)(2,1)} fusion(bf16[2,1024,6,128]{3,1,2,0:T(8,128)(2,1)S(1)} %copy.159, s32[1024]{0:T(1024)S(1)} %pad_clamp_fusion), kind=kCustom, calls=%fused_computation.1 | custom fusion | bytes 6291480 | tf_op jit(solution)/shard_map/jit(_take)/gather | solution.py:55
  38.3 3.4 %copy.160 = bf16[2,1024,6,128]{1,3,2,0:T(8,128)(2,1)S(1)} copy(bf16[2,1024,6,128]{3,1,0,2:T(8,128)(2,1)} %bitcast.69) | data formatting | bytes 6291456 | tf_op jit(solution)/shard_map/jit(_take)/gather | solution.py:55
  41.7 0.3 bitcast_select_fusion
  42.0 0.7 copy-done
  42.7 0.5 copy-done.1
  43.3 1.7 multiply_reduce_fusion
  44.9 0.5 divide_convert_fusion
  45.5 0.9 convolution_convert_fusion.7
  46.4 1.0 subtract_convert_fusion.7
  47.4 0.9 convolution_convert_fusion.6
  48.3 1.0 subtract_convert_fusion.6
  49.3 0.9 convolution_convert_fusion.5
  50.2 1.0 subtract_convert_fusion.5
  51.2 0.9 convolution_convert_fusion.4
  52.2 1.0 subtract_convert_fusion.4
  53.1 0.9 convolution_convert_fusion.3
  54.1 1.0 subtract_convert_fusion.3
  55.1 0.9 convolution_convert_fusion.2
  56.0 1.2 subtract_convert_fusion.2
  57.2 0.9 convolution_convert_fusion.1
  58.1 1.0 subtract_convert_fusion.1
  59.1 0.9 convolution_convert_fusion
  60.1 1.0 subtract_convert_fusion
  61.1 4.5 %fusion.10 = f32[2,2,384,1024]{3,2,1,0:T(8,128)} fusion(bf16[2,1024,2,384]{1,3,2,0:T(8,128)(2,1)S(1)} %bitcast_select_fusion, bf16[2,2,384,384]{2,3,0,1:T(8,128)(2,1)S(1)} %subtract_convert_fusion), kind=kOutput, calls=%fused_computation.36 | convolution fusion | flops 1207959552 | bytes 10616832 | tf_op jit(solution)/shard_map/sfka,skab->sfkb/dot_general | solution.py:74
  65.6 8.2 %copy.197 = f32[2,1024,6,128]{3,2,1,0:T(8,128)} copy(f32[2,1024,6,128]{1,3,2,0:T(8,128)} %bitcast.66) | data formatting | bytes 12582912 | tf_op jit(solution)/shard_map/reshape | solution.py:77
  73.8 10.4 %convolution_reduce_fusion = f32[6,1024,128]{2,0,1:T(8,128)} fusion(f32[2,1024,6,128]{3,2,1,0:T(8,128)} %copy.197, s32[6]{0:T(128)S(1)} %eq.40), kind=kOutput, calls=%fused_computation.6 | convolution fusion | flops 114032672 | bytes 9437208 | tf_op jit(solution)/shard_map/sfjc,jw->sfwc/dot_general | solution.py:81
  84.2 3.7 %copy.198 = f32[1024,6,128]{0,2,1:T(8,128)S(1)} copy(f32[1024,6,128]{2,1,0:T(8,128)} %bitcast.70) | data formatting | bytes 6291456 | tf_op jit(solution)/shard_map/reduce_sum | solution.py:87
  87.9 0.2 bitcast_convert_fusion
  88.2 1.0 slice_bitcast_fusion.2
  89.2 7.5 %collective-permute-start.4 = (bf16[1024,256]{0,1:T(8,128)(2,1)}, bf16[1024,256]{0,1:T(8,128)(2,1)}, u32[]{:S(2)}, u32[]{:S(2)}) collective-permute-start(bf16[1024,256]{0,1:T(8,128)(2,1)} %get-tuple-element.7), channel_id=1, source_target_pairs={{0,1},{1,2},{2,3},{3,4},{4,5},{5,6},{6,7},{8,9},{9,10},{10,11},{11... | collective-permute-start | bytes 1572872 | tf_op jit(solution)/shard_map/ppermute | solution.py:33
  96.7 1.3 collective-permute-start.5
  98.1 2.4 %collective-permute-start.7 = (s32[2,3]{0,1:T(4,128)S(1)}, s32[2,3]{0,1:T(4,128)S(1)}, u32[]{:S(2)}, u32[]{:S(2)}) collective-permute-start(s32[2,3]{0,1:T(4,128)S(1)} %collective-permute-done.6), channel_id=1, source_target_pairs={{0,1},{1,2},{2,3},{3,4},{4,5},{5,6},{6,7},{7,0},{8,9},{9,10},{10,1... | collective-permute-start | bytes 80 | tf_op jit(solution)/shard_map/ppermute | solution.py:44
  100.4 4.1 %collective-permute-done.7 = s32[2,3]{0,1:T(4,128)S(1)} collective-permute-done((s32[2,3]{0,1:T(4,128)S(1)}, s32[2,3]{0,1:T(4,128)S(1)}, u32[]{:S(2)}, u32[]{:S(2)}) %collective-permute-start.7) | collective-permute-done | bytes 56 | tf_op jit(solution)/shard_map/ppermute | solution.py:44
  104.5 0.3 collective-permute-start.8
  104.8 4.5 %collective-permute-done.8 = s32[2,3]{0,1:T(4,128)S(1)} collective-permute-done((s32[2,3]{0,1:T(4,128)S(1)}, s32[2,3]{0,1:T(4,128)S(1)}, u32[]{:S(2)}, u32[]{:S(2)}) %collective-permute-start.8) | collective-permute-done | bytes 56 | tf_op jit(solution)/shard_map/ppermute | solution.py:44
  109.4 4.8 %collective-permute-done.9 = s32[2,3]{0,1:T(4,128)S(1)} collective-permute-done((s32[2,3]{0,1:T(4,128)S(1)}, s32[2,3]{0,1:T(4,128)S(1)}, u32[]{:S(2)}, u32[]{:S(2)}) %collective-permute-start.9) | collective-permute-done | bytes 56 | tf_op jit(solution)/shard_map/ppermute | solution.py:44
  114.2 4.8 %collective-permute-done.10 = s32[2,3]{0,1:T(4,128)S(1)} collective-permute-done((s32[2,3]{0,1:T(4,128)S(1)}, s32[2,3]{0,1:T(4,128)S(1)}, u32[]{:S(2)}, u32[]{:S(2)}) %collective-permute-start.10) | collective-permute-done | bytes 56 | tf_op jit(solution)/shard_map/ppermute | solution.py:44
  119.0 4.8 %collective-permute-done.11 = s32[2,3]{0,1:T(4,128)S(1)} collective-permute-done((s32[2,3]{0,1:T(4,128)S(1)}, s32[2,3]{0,1:T(4,128)S(1)}, u32[]{:S(2)}, u32[]{:S(2)}) %collective-permute-start.11) | collective-permute-done | bytes 56 | tf_op jit(solution)/shard_map/ppermute | solution.py:44
  123.8 4.8 %collective-permute-done.12 = s32[2,3]{0,1:T(4,128)S(1)} collective-permute-done((s32[2,3]{0,1:T(4,128)S(1)}, s32[2,3]{0,1:T(4,128)S(1)}, u32[]{:S(2)}, u32[]{:S(2)}) %collective-permute-start.12) | collective-permute-done | bytes 56 | tf_op jit(solution)/shard_map/ppermute | solution.py:44
  128.6 0.1 concatenate.14
  128.8 0.1 copy.202
  128.9 0.1 eq.45
  129.0 0.2 fusion.28
  129.2 2.4 %fusion.23 = f32[1024,256]{0,1:T(8,128)} fusion(f32[1024,3,256]{0,2,1:T(8,128)S(1)} %bitcast.68, bf16[1024,256]{0,1:T(8,128)(2,1)} %collective-permute-done.5, bf16[1024,256]{0,1:T(8,128)(2,1)} %collective-permute-done.4, f32[256]{0:T(256)S(1)} %broadcast_bitcast_fusion.1), kind=kLoop, calls=%fused_computation.50 | loop fusion | flops 1310720 | bytes 3146752 | tf_op jit(solution)/shard_map/div | solution.py:95
  131.7 50.8 %all-reduce.2.cloned.1.call-done = f32[1024,256]{0,1:T(8,128)} async-done(((f32[1024,256]{0,1:T(8,128)}), f32[1024,256]{0,1:T(8,128)}) %all-reduce.2.cloned.1.call-update) | async-done | bytes 1048592 | tf_op jit(solution)/shard_map/psum | solution.py:96
  182.5 1.3 broadcast_multiply_fusion
  183.8 1.3 copy.203
  (31 shorter events, 0.5 us)
Async XLA Ops:
  6.5 6.5 %copy-start.2 = (bf16[2,1024,256]{2,1,0:T(8,128)(2,1)S(1)}, bf16[2,1024,256]{2,1,0:T(8,128)(2,1)}, u32[]{:S(2)}) copy-start(bf16[2,1024,256]{2,1,0:T(8,128)(2,1)} %param.3) | copy-start | bytes 3145732
  6.5 14.5 %copy-start.4 = (s32[2,3]{1,0:T(2,128)S(1)}, s32[2,3]{1,0:T(2,128)}, u32[]{:S(2)}) copy-start(s32[2,3]{1,0:T(2,128)} %param.5) | copy-start | bytes 76
  6.5 176.0 %all-reduce.2.cloned.1.call-start = ((), (), s32[]{:S(2)}) async-start(), calls=%async_computation | async-start | bytes 2097152 | tf_op jit(solution)/shard_map/psum | solution.py:96
  7.9 15.1 %collective-permute-start.1 = (bf16[1024,256]{0,1:T(8,128)(2,1)S(1)}, bf16[1024,256]{0,1:T(8,128)(2,1)S(1)}, u32[]{:S(2)}, u32[]{:S(2)}) collective-permute-start(bf16[1024,256]{0,1:T(8,128)(2,1)S(1)} %copy.151), channel_id=1, source_target_pairs={{1,0},{2,1},{3,2},{4,3},{5,4},{6,5},{7,6},{9,8},{10,9},{11,10},{12... | collective-permute-start | bytes 1572872 | tf_op jit(solution)/shard_map/ppermute | solution.py:23
  9.2 14.6 %collective-permute-start = (bf16[1024,256]{0,1:T(8,128)(2,1)S(1)}, bf16[1024,256]{0,1:T(8,128)(2,1)}, u32[]{:S(2)}, u32[]{:S(2)}) collective-permute-start(bf16[1024,256]{0,1:T(8,128)(2,1)S(1)} %copy.151), channel_id=1, source_target_pairs={{0,1},{1,2},{2,3},{3,4},{4,5},{5,6},{6,7},{8,9},{9,10},{10,11},{11... | collective-permute-start | bytes 1572872 | tf_op jit(solution)/shard_map/ppermute | solution.py:21
  14.3 14.6 %collective-permute-start.3 = (bf16[2,1024,256]{1,2,0:T(8,128)(2,1)}, bf16[2,1024,256]{1,2,0:T(8,128)(2,1)}, u32[]{:S(2)}, u32[]{:S(2)}) collective-permute-start(bf16[2,1024,256]{1,2,0:T(8,128)(2,1)} %copy.156), channel_id=1, source_target_pairs={{1,0},{2,1},{3,2},{4,3},{5,4},{6,5},{7,6},{9,8},{10,9},{11,10},{12... | collective-permute-start | bytes 3145736 | tf_op jit(solution)/shard_map/ppermute | solution.py:23
  15.6 13.4 %collective-permute-start.2 = (bf16[2,1024,256]{1,2,0:T(8,128)(2,1)}, bf16[2,1024,256]{1,2,0:T(8,128)(2,1)}, u32[]{:S(2)}, u32[]{:S(2)}) collective-permute-start(bf16[2,1024,256]{1,2,0:T(8,128)(2,1)} %copy.156), channel_id=1, source_target_pairs={{0,1},{1,2},{2,3},{3,4},{4,5},{5,6},{6,7},{8,9},{9,10},{10,11},{11... | collective-permute-start | bytes 3145736 | tf_op jit(solution)/shard_map/ppermute | solution.py:21
  21.1 76.9 %collective-permute-start.6 = (s32[2,3]{0,1:T(4,128)S(1)}, s32[2,3]{0,1:T(4,128)S(1)}, u32[]{:S(2)}, u32[]{:S(2)}) collective-permute-start(s32[2,3]{0,1:T(4,128)S(1)} %copy.199), channel_id=1, source_target_pairs={{0,1},{1,2},{2,3},{3,4},{4,5},{5,6},{6,7},{7,0},{8,9},{9,10},{10,1... | collective-permute-start | bytes 80 | tf_op jit(solution)/shard_map/ppermute | solution.py:44
  23.0 0.8 copy-start.3
  41.7 1.1 copy-start
  41.7 1.6 copy-start.1
  89.2 40.0 %collective-permute-start.4 = (bf16[1024,256]{0,1:T(8,128)(2,1)}, bf16[1024,256]{0,1:T(8,128)(2,1)}, u32[]{:S(2)}, u32[]{:S(2)}) collective-permute-start(bf16[1024,256]{0,1:T(8,128)(2,1)} %get-tuple-element.7), channel_id=1, source_target_pairs={{0,1},{1,2},{2,3},{3,4},{4,5},{5,6},{6,7},{8,9},{9,10},{10,11},{11... | collective-permute-start | bytes 1572872 | tf_op jit(solution)/shard_map/ppermute | solution.py:33
  96.7 32.5 %collective-permute-start.5 = (bf16[1024,256]{0,1:T(8,128)(2,1)}, bf16[1024,256]{0,1:T(8,128)(2,1)}, u32[]{:S(2)}, u32[]{:S(2)}) collective-permute-start(bf16[1024,256]{0,1:T(8,128)(2,1)} %get-tuple-element.8), channel_id=1, source_target_pairs={{1,0},{2,1},{3,2},{4,3},{5,4},{6,5},{7,6},{9,8},{10,9},{11,10},{12... | collective-permute-start | bytes 1572872 | tf_op jit(solution)/shard_map/ppermute | solution.py:33
  98.1 6.5 %collective-permute-start.7 = (s32[2,3]{0,1:T(4,128)S(1)}, s32[2,3]{0,1:T(4,128)S(1)}, u32[]{:S(2)}, u32[]{:S(2)}) collective-permute-start(s32[2,3]{0,1:T(4,128)S(1)} %collective-permute-done.6), channel_id=1, source_target_pairs={{0,1},{1,2},{2,3},{3,4},{4,5},{5,6},{6,7},{7,0},{8,9},{9,10},{10,1... | collective-permute-start | bytes 80 | tf_op jit(solution)/shard_map/ppermute | solution.py:44
  104.5 4.8 %collective-permute-start.8 = (s32[2,3]{0,1:T(4,128)S(1)}, s32[2,3]{0,1:T(4,128)S(1)}, u32[]{:S(2)}, u32[]{:S(2)}) collective-permute-start(s32[2,3]{0,1:T(4,128)S(1)} %collective-permute-done.7), channel_id=1, source_target_pairs={{0,1},{1,2},{2,3},{3,4},{4,5},{5,6},{6,7},{7,0},{8,9},{9,10},{10,1... | collective-permute-start | bytes 80 | tf_op jit(solution)/shard_map/ppermute | solution.py:44
  109.4 4.8 %collective-permute-start.9 = (s32[2,3]{0,1:T(4,128)S(1)}, s32[2,3]{0,1:T(4,128)S(1)}, u32[]{:S(2)}, u32[]{:S(2)}) collective-permute-start(s32[2,3]{0,1:T(4,128)S(1)} %collective-permute-done.8), channel_id=1, source_target_pairs={{0,1},{1,2},{2,3},{3,4},{4,5},{5,6},{6,7},{7,0},{8,9},{9,10},{10,1... | collective-permute-start | bytes 80 | tf_op jit(solution)/shard_map/ppermute | solution.py:44
  114.2 4.8 %collective-permute-start.10 = (s32[2,3]{0,1:T(4,128)S(1)}, s32[2,3]{0,1:T(4,128)S(1)}, u32[]{:S(2)}, u32[]{:S(2)}) collective-permute-start(s32[2,3]{0,1:T(4,128)S(1)} %collective-permute-done.9), channel_id=1, source_target_pairs={{0,1},{1,2},{2,3},{3,4},{4,5},{5,6},{6,7},{7,0},{8,9},{9,10},{10,1... | collective-permute-start | bytes 80 | tf_op jit(solution)/shard_map/ppermute | solution.py:44
  119.0 4.8 %collective-permute-start.11 = (s32[2,3]{0,1:T(4,128)S(1)}, s32[2,3]{0,1:T(4,128)S(1)}, u32[]{:S(2)}, u32[]{:S(2)}) collective-permute-start(s32[2,3]{0,1:T(4,128)S(1)} %collective-permute-done.10), channel_id=1, source_target_pairs={{0,1},{1,2},{2,3},{3,4},{4,5},{5,6},{6,7},{7,0},{8,9},{9,10},{10,1... | collective-permute-start | bytes 80 | tf_op jit(solution)/shard_map/ppermute | solution.py:44
  123.8 4.8 %collective-permute-start.12 = (s32[2,3]{0,1:T(4,128)S(1)}, s32[2,3]{0,1:T(4,128)S(1)}, u32[]{:S(2)}, u32[]{:S(2)}) collective-permute-start(s32[2,3]{0,1:T(4,128)S(1)} %collective-permute-done.11), channel_id=1, source_target_pairs={{0,1},{1,2},{2,3},{3,4},{4,5},{5,6},{6,7},{7,0},{8,9},{9,10},{10,1... | collective-permute-start | bytes 80 | tf_op jit(solution)/shard_map/ppermute | solution.py:44
Sparse Core Ops, SparseCore 0:
  131.8 50.6 all-reduce.1
